TPU v7x, 8 devices: a whole 2x2x1 slice. The times are simulated.
8 devices in a mesh: tp: 2 (over z, y), ep: 4 (over x, core).
Axes of the slice: x: 2, y: 2, z: 1, core: 2. Of those that a mesh axis runs over, the one named last changes fastest.
Arguments:
- x: bfloat16 [4096, 2048], P(('ep', 'tp'))
- idx: int32 [4096, 4], P(('ep', 'tp'))
- g: float32 [4096, 4], P(('ep', 'tp'))
- slot: int32 [4096, 4], P(('ep', 'tp'))
- ws1: bfloat16 [2048, 5632], P(None, 'tp')
- ws3: bfloat16 [2048, 5632], P(None, 'tp')
- ws2: bfloat16 [5632, 2048], P('tp')
- w1: bfloat16 [60, 2048, 1408], P('ep')
- w3: bfloat16 [60, 2048, 1408], P('ep')
- w2: bfloat16 [60, 1408, 2048], P('ep')
Outputs:
- output: bfloat16 [4096, 2048], P(('ep', 'tp'))
All inputs are finite; a program needn't handle non-finite values.
Results may differ from a plain program's by a relative error of at most 0.001.
Values are sent between devices in bfloat16 or wider.
A program may use at most 1.25 GiB of HBM per device.

v0:
```python
import functools

import jax
import jax.numpy as jnp
from jax import lax
from jax.experimental import pallas as pl
from jax.experimental.pallas import tpu as pltpu
from jax.sharding import PartitionSpec as P

CAP = 72
MAIN = 64
TAIL = CAP - MAIN
MIB = 1024 * 1024
ANY = pl.BlockSpec(memory_space=pl.ANY)


def _params(mib):
    return pltpu.CompilerParams(vmem_limit_bytes=mib * MIB)


def _dot(a, b):
    return jnp.dot(a, b, preferred_element_type=jnp.float32)


def _hot(c, n, base, tok):
    r = (lax.broadcasted_iota(jnp.int32, (n, tok), 0) + base).astype(jnp.float32)
    hit = r == c[0:1, :]
    for j in range(1, 4):
        hit = hit | (r == c[j:j + 1, :])
    return jnp.where(hit, 1.0, 0.0).astype(jnp.bfloat16)


def _codes(t, me, el):
    code = t[0:4, :].astype(jnp.int32)
    e, k = code >> 7, code & 127
    le = e - me * el
    ok = (code >= 0) & (le >= 0) & (le < el)
    c = jnp.where(ok, jnp.where(k < MAIN, le * MAIN + k, el * MAIN + le * TAIL + k - MAIN), -1).astype(jnp.float32)
    g = t[4:8, :]
    g0 = g.astype(jnp.bfloat16).astype(jnp.float32)
    g1 = (g - g0).astype(jnp.bfloat16).astype(jnp.float32)
    return c, jnp.concatenate([c, g0, g1, g - g0 - g1], axis=0)


def _front_kernel(el, kt, x, mine, w1, w3, w2, cx, gm, base, sy, xc, xx, xxc,
                  y, tabs, tabt, v1, v3, v2, hs, sst, gst, wsem, xsend, xrecv, tsend, trecv, ssem, gsem):
    me = lax.axis_index("ep")
    tp = lax.axis_index("tp")
    sib = me + 1 - 2 * lax.rem(me, 2)
    peer = lax.rem(me + 2, 4)
    diag = lax.rem(sib + 2, 4)
    tok, d = x.shape
    half = tok // 2
    nf, nn = v1.shape[0], v2.shape[0]
    tf, tn = v1.shape[2], v2.shape[2]
    mesh_id = pl.DeviceIdType.MESH

    def remote(src, dst, ss, rs, dev):
        return pltpu.make_async_remote_copy(src, dst, ss, rs, device_id=dev, device_id_type=mesh_id)

    def up(i):
        col = pl.ds(pl.multiple_of(i * tf, tf), tf)
        return (pltpu.make_async_copy(w1.at[:, col], v1.at[i], wsem.at[i]),
                pltpu.make_async_copy(w3.at[:, col], v3.at[i], wsem.at[nf + i]))

    def down(i):
        return pltpu.make_async_copy(w2.at[:, pl.ds(pl.multiple_of(i * tn, tn), tn)], v2.at[i], wsem.at[2 * nf + i])

    barrier = pltpu.get_barrier_semaphore()
    for dev in (sib, peer, diag):
        pl.semaphore_signal(barrier, inc=1, device_id={"ep": dev}, device_id_type=mesh_id)
    pl.semaphore_signal(barrier, inc=1, device_id={"tp": 1 - tp}, device_id_type=mesh_id)
    pl.semaphore_wait(barrier, 4)
    tcopy = [remote(mine, tabs.at[k], tsend.at[k], trecv.at[k], {"ep": dev}) for k, dev in enumerate((sib, peer, diag))]
    xcopy = remote(x, xx, xsend.at[0], xrecv.at[0], {"ep": peer})
    ccopy = remote(x, xc, xsend.at[1], xrecv.at[1], {"ep": sib})
    ycopy = [remote(x.at[pl.ds(k * half, half)], y.at[pl.ds(k * half, half)], xsend.at[2 + k], xrecv.at[2 + k], {"tp": 1 - tp})
             for k in range(2)]
    relay = remote(xx, xxc, xsend.at[4], xrecv.at[4], {"ep": sib})
    for c in (*tcopy, xcopy, *ycopy, ccopy):
        c.start()
    for i in range(nf):
        for c in up(i):
            c.start()
    for i in range(nn):
        down(i).start()

    def store_tab(s, tab):
        wide = jnp.concatenate([tab, jnp.zeros((128 - tab.shape[0], tok), jnp.float32)], axis=0)
        for b in range(0, tok, 128):
            tabt[s * tok + b:s * tok + b + 128, :] = jnp.transpose(wide[:, b:b + 128])

    def shared(src, lo, n, out, add, first):
        scopy = lambda i: pltpu.make_async_copy(
            sst.at[lax.rem(i, 2), pl.ds(0, n)], out.at[pl.ds(lo, n), pl.ds(pl.multiple_of(i * tn, tn), tn)], ssem.at[lax.rem(i, 2)])

        def gate(i, _):
            if first:
                for c in up(i):
                    c.wait()
            r = src[lo:lo + n, :]
            a = _dot(r, v1[i])
            b = _dot(r, v3[i])
            hs[lo:lo + n, pl.ds(pl.multiple_of(i * tf, tf), tf)] = (jax.nn.silu(a) * b).astype(jnp.bfloat16)
            return 0

        def tile(i, _):
            if first:
                down(i).wait()

            @pl.when(i >= 2)
            def _():
                scopy(i - 2).wait()

            r = _dot(hs[lo:lo + n, :], v2[i])
            if add:
                r = r + src[lo:lo + n, pl.ds(pl.multiple_of(i * tn, tn), tn)].astype(jnp.float32)
            sst[lax.rem(i, 2), 0:n, :] = r
            scopy(i).start()
            return 0

        lax.fori_loop(0, nf, gate, 0)
        lax.fori_loop(0, nn, tile, 0)
        for i in (nn - 2, nn - 1):
            scopy(jnp.int32(i)).wait()

    shared(x, 0, tok, base, True, True)
    for k in range(4):
        if k:
            tcopy[k - 1].wait()
        c, tab = _codes(mine[...] if k == 0 else tabs[k - 1], me, el)
        cx[k] = jnp.concatenate([c, c], axis=0)
        store_tab(k, tab)

    blk = gst.shape[1]
    gcopy = lambda i: pltpu.make_async_copy(gst.at[lax.rem(i, 2)], gm.at[pl.ds(pl.multiple_of(i * blk, blk), blk)], gsem.at[lax.rem(i, 2)])

    def gates(i, _):
        @pl.when(i >= 2)
        def _():
            gcopy(i - 2).wait()

        t = tabt[pl.ds(pl.multiple_of(i * blk, blk), blk), :]
        lane = lax.broadcasted_iota(jnp.int32, (blk, kt), 1).astype(jnp.float32)
        acc = [jnp.zeros((blk, kt), jnp.float32) for _ in range(3)]
        for j in range(4):
            hit = t[:, j:j + 1] == lane
            for q in range(3):
                acc[q] = jnp.where(hit, t[:, 4 + 4 * q + j:5 + 4 * q + j], acc[q])
        for q in range(3):
            gst[lax.rem(i, 2), :, q * kt:(q + 1) * kt] = acc[q].astype(jnp.bfloat16)
        gcopy(i).start()
        return 0

    ng = 4 * tok // blk
    lax.fori_loop(0, ng, gates, 0)
    for i in (ng - 2, ng - 1):
        gcopy(jnp.int32(i)).wait()
    ycopy[0].wait()
    shared(y, 0, half, sy, False, False)
    xcopy.wait()
    relay.start()
    ycopy[1].wait()
    shared(y, half, half, sy, False, False)
    ccopy.wait()
    relay.wait()


def _front(x, mine, w1, w3, w2, el, kt):
    tok, d = x.shape
    f = w1.shape[1]
    tf, tn = 256, 256
    nf, nn = f // tf, d // tn
    bf16, f32 = jnp.bfloat16, jnp.float32
    vmem = pl.BlockSpec(memory_space=pltpu.VMEM)
    dma = pltpu.SemaphoreType.DMA
    return pl.pallas_call(
        functools.partial(_front_kernel, el, kt),
        out_shape=[jax.ShapeDtypeStruct(sh, dt) for sh, dt in (
            ((4, 8, tok), f32), ((4 * tok, 3 * kt), bf16), ((tok, d), f32), ((tok, d), f32),
            ((tok, d), bf16), ((tok, d), bf16), ((tok, d), bf16))],
        in_specs=[vmem, vmem] + [ANY] * 3,
        out_specs=[vmem] + [ANY] * 6,
        scratch_shapes=[
            pltpu.VMEM((tok, d), bf16),
            pltpu.VMEM((3, 8, tok), f32),
            pltpu.VMEM((4 * tok, 128), f32),
            pltpu.VMEM((nf, d, tf), bf16),
            pltpu.VMEM((nf, d, tf), bf16),
            pltpu.VMEM((nn, f, tn), bf16),
            pltpu.VMEM((tok, f), bf16),
            pltpu.VMEM((2, tok, tn), f32),
            pltpu.VMEM((2, 128, 3 * kt), bf16),
            dma((2 * nf + nn,)), dma((5,)), dma((5,)), dma((3,)), dma((3,)), dma((2,)), dma((2,)),
        ],
        compiler_params=pltpu.CompilerParams(vmem_limit_bytes=62 * MIB, collective_id=1, has_side_effects=True),
        cost_estimate=pl.CostEstimate(flops=12 * tok * d * f, bytes_accessed=6 * d * f, transcendentals=0),
        name="front",
    )(x, mine, w1, w3, w2)


def _up_kernel(el, x0, x1, x2, x3, cx, w1, w3, h, xs, tg, xb, wv, xsem, wsem):
    e = pl.program_id(0)
    tok, d = x0.shape
    ring = wv.shape[0]
    srcs = (x0, x1, x2, x3)
    some = 5

    def wcopy(w, i, k):
        slot = lax.rem(2 * i + k, ring)
        return pltpu.make_async_copy(w.at[i], wv.at[slot], wsem.at[slot])

    xcopy = lambda s, k: pltpu.make_async_copy(srcs[s], xb.at[k], xsem.at[k])

    @pl.when(e == 0)
    def _():
        xcopy(0, 0).start()
        xcopy(1, 1).start()
        for i in range(ring):
            wcopy(w3 if i % 2 else w1, jnp.int32(i // 2), i % 2).start()

        def select(s, _):
            k = lax.rem(s, 2)
            xcopy(0, k).wait()
            c = cx[s]
            for b in range(0, el, some):
                p = _hot(c, some * MAIN, b * MAIN, tok)
                for n in range(0, d, 512):
                    r = _dot(p, xb[k, :, n:n + 512]).astype(jnp.bfloat16)
                    for i in range(some):
                        xs[b + i, pl.ds(pl.multiple_of(s * MAIN, MAIN), MAIN), n:n + 512] = r[i * MAIN:(i + 1) * MAIN]
            p = _hot(c, el * TAIL, el * MAIN, tok)
            for n in range(0, d, 512):
                tg[s, :, n:n + 512] = _dot(p, xb[k, :, n:n + 512])
            for j in range(2):
                @pl.when(s == j)
                def _(j=j):
                    xcopy(2 + j, j).start()
            return 0

        lax.fori_loop(0, 4, select, 0)

    tail = pl.ds(pl.multiple_of(e * TAIL, TAIL), TAIL)
    xs[e, 4 * MAIN:4 * CAP, :] = jnp.concatenate([tg[s, tail, :] for s in range(4)], axis=0).astype(jnp.bfloat16)
    f = h.shape[-1]
    full = f // 256 * 256
    wcopy(w1, e, 0).wait()
    wcopy(w3, e, 1).wait()
    x = xs[e]
    v1, v3 = wv.at[lax.rem(2 * e, ring)], wv.at[lax.rem(2 * e + 1, ring)]
    for n in range(0, full, 256):
        a = _dot(x, v1[:, n:n + 256])
        b = _dot(x, v3[:, n:n + 256])
        h[0, :, n:n + 256] = (jax.nn.silu(a) * b).astype(jnp.bfloat16)
    if full < f:
        r = f - full
        ab = _dot(x, jnp.concatenate([v1[:, full:], v3[:, full:]], axis=1))
        h[0, :, full:] = (jax.nn.silu(ab[:, :r]) * ab[:, r:]).astype(jnp.bfloat16)

    @pl.when(e + 2 < el)
    def _():
        wcopy(w3, e + 2, 1).start()

    @pl.when(e + 3 < el)
    def _():
        wcopy(w1, e + 3, 0).start()


def _up(xs, cx, w1, w3):
    el, d, f = w1.shape
    tok = xs[0].shape[0]
    ring = 5
    return pl.pallas_call(
        functools.partial(_up_kernel, el),
        grid=(el,),
        out_shape=jax.ShapeDtypeStruct((el, 4 * CAP, f), jnp.bfloat16),
        in_specs=[ANY] * 4 + [pl.BlockSpec(cx.shape, lambda e: (0, 0, 0))] + [ANY] * 2,
        out_specs=pl.BlockSpec((1, 4 * CAP, f), lambda e: (e, 0, 0)),
        scratch_shapes=[
            pltpu.VMEM((el, 4 * CAP, d), jnp.bfloat16),
            pltpu.VMEM((4, el * TAIL, d), jnp.float32),
            pltpu.VMEM((2, tok, d), jnp.bfloat16),
            pltpu.VMEM((ring, d, f), jnp.bfloat16),
            pltpu.SemaphoreType.DMA((2,)),
            pltpu.SemaphoreType.DMA((ring,)),
        ],
        compiler_params=_params(63),
        cost_estimate=pl.CostEstimate(flops=2 * 2 * el * 4 * CAP * d * f, bytes_accessed=4 * el * d * f, transcendentals=0),
        name="up",
    )(*xs, cx, w1, w3)


def _route_kernel(el, tok, cols, g, h, w2, base, sy, out, gv, hv, wv, r3, rt, send, recv, far, own, back, yb, bv, ost,
                  gsem, hsem, wsem, ssem, rsem, xssem, xrsem, osem, yssem, yrsem, bsem):
    me = lax.axis_index("ep")
    tp = lax.axis_index("tp")
    sib = me + 1 - 2 * lax.rem(me, 2)
    peer = lax.rem(me + 2, 4)
    ring = wv.shape[0]
    chunks = back.shape[0]
    kt = gv.shape[1] // 3
    nm = el * MAIN
    total = chunks * el
    unroll = 5

    gcopy = lambda s: pltpu.make_async_copy(g.at[pl.ds(s * tok, tok)], gv.at[pl.ds(s * tok, tok)], gsem.at[s])
    hcopy = lambda e: pltpu.make_async_copy(h.at[e], hv.at[e], hsem.at[e])

    def wcopy(t):
        slot = lax.rem(t, ring)
        col = pl.multiple_of(t // el * cols, cols)
        return pltpu.make_async_copy(w2.at[lax.rem(t, el), :, pl.ds(col, cols)], wv.at[slot], wsem.at[slot])

    def pair(c, k):
        return pltpu.make_async_remote_copy(send.at[lax.rem(c, 2), k], recv.at[c, k], ssem.at[c, k], rsem.at[c, k],
                                            device_id={"ep": sib}, device_id_type=pl.DeviceIdType.MESH)

    def across(c):
        return pltpu.make_async_remote_copy(recv.at[c, 1], back.at[c], xssem.at[c], xrsem.at[c],
                                            device_id={"ep": peer}, device_id_type=pl.DeviceIdType.MESH)

    part = lambda ref, c: ref.at[:, pl.ds(pl.multiple_of(c * cols, cols), cols)]

    def ycopy(c):
        return pltpu.make_async_remote_copy(part(sy, c), yb.at[c], yssem.at[c], yrsem.at[c],
                                            device_id={"tp": 1 - tp}, device_id_type=pl.DeviceIdType.MESH)

    bcopy = lambda c: pltpu.make_async_copy(part(base, c), bv.at[lax.rem(c, 2)], bsem.at[lax.rem(c, 2)])
    ocopy = lambda c: pltpu.make_async_copy(ost.at[lax.rem(c, 2)], part(out, c), osem.at[lax.rem(c, 2)])

    for e in range(el):
        hcopy(e).start()
        if e < ring:
            wcopy(jnp.int32(e)).start()
    for s in (3, 1, 2, 0):
        gcopy(s).start()
    barrier = pltpu.get_barrier_semaphore()
    for dev in (sib, peer):
        pl.semaphore_signal(barrier, inc=1, device_id={"ep": dev}, device_id_type=pl.DeviceIdType.MESH)
    pl.semaphore_signal(barrier, inc=1, device_id={"tp": 1 - tp}, device_id_type=pl.DeviceIdType.MESH)
    pl.semaphore_wait(barrier, 3)
    for c in range(chunks):
        ycopy(jnp.int32(c)).start()
    for c in range(2):
        bcopy(jnp.int32(c)).start()

    def group(c, k):
        for u in range(unroll):
            t = c * el + k * unroll + u
            wcopy(t).wait()

            @pl.when(c == 0)
            def _():
                hcopy(k * unroll + u).wait()

        for u in range(unroll):
            e = k * unroll + u
            r = _dot(hv[e], wv[lax.rem(c * el + e, ring)]).astype(jnp.bfloat16)
            row = pl.multiple_of(e * MAIN, MAIN)
            for s in range(4):
                for i in range(3):
                    r3[s, pl.ds(row + i * kt, MAIN), :] = r[s * MAIN:(s + 1) * MAIN]
            q = r[4 * MAIN:].astype(jnp.float32)
            for s in range(4):
                rt[s, pl.ds(pl.multiple_of(e * TAIL, TAIL), TAIL), :] = q[s * TAIL:(s + 1) * TAIL]
        for u in range(unroll):
            t = c * el + k * unroll + u

            @pl.when(t + ring < total)
            def _():
                wcopy(t + ring).start()

    def combine(s):
        tail = jnp.concatenate([rt[s], jnp.zeros((kt - el * CAP, cols), jnp.float32)], axis=0).astype(jnp.bfloat16)
        for i in range(3):
            r3[s, i * kt + nm:(i + 1) * kt, :] = tail
        return _dot(gv[s * tok:(s + 1) * tok, :], r3[s])

    def merge(c):
        pair(c, 1).wait_recv()
        recv[c, 1] = recv[c, 1] + far[...]
        pair(c, 0).wait_recv()
        recv[c, 0] = recv[c, 0] + own[...]
        across(c).start()

    def chunk(c, _):
        def step(k, _):
            group(c, k)

            @pl.when((k == 0) & (c > 0))
            def _():
                merge(c - 1)

            return 0

        lax.fori_loop(0, el // unroll, step, 0)

        @pl.when(c == 0)
        def _():
            for s in range(4):
                gcopy(s).wait()

        @pl.when(c >= 2)
        def _():
            pair(c - 2, 0).wait_send()
            pair(c - 2, 1).wait_send()

        slot = lax.rem(c, 2)
        send[slot, 1] = combine(3)
        send[slot, 0] = combine(1)
        pair(c, 1).start()
        far[...] = combine(2)
        pair(c, 0).start()
        own[...] = combine(0)
        return 0

    lax.fori_loop(0, chunks, chunk, 0)
    merge(jnp.int32(chunks - 1))

    def finish(c, _):
        k = lax.rem(c, 2)
        bcopy(c).wait()
        ycopy(c).wait_recv()

        @pl.when(c >= 2)
        def _():
            ocopy(c - 2).wait()

        across(c).wait_recv()
        ost[k] = (bv[k] + yb[c] + (recv[c, 0] + back[c])).astype(jnp.bfloat16)
        ocopy(c).start()

        @pl.when(c + 2 < chunks)
        def _():
            bcopy(c + 2).start()

        return 0

    lax.fori_loop(0, chunks, finish, 0)
    for c in range(chunks - 2, chunks):
        pair(jnp.int32(c), 0).wait_send()
        pair(jnp.int32(c), 1).wait_send()
        ocopy(jnp.int32(c)).wait()
    for c in range(chunks):
        across(jnp.int32(c)).wait_send()
        ycopy(jnp.int32(c)).wait_send()


def _route(g, h, w2, base, sy):
    el, f, d = w2.shape
    tok = base.shape[0]
    cols = 256
    chunks = d // cols
    ring = 8
    k3 = g.shape[1]
    f32 = jnp.float32
    return pl.pallas_call(
        functools.partial(_route_kernel, el, tok, cols),
        out_shape=jax.ShapeDtypeStruct((tok, d), jnp.bfloat16),
        in_specs=[ANY] * 5,
        out_specs=ANY,
        scratch_shapes=[
            pltpu.VMEM((4 * tok, k3), jnp.bfloat16),
            pltpu.VMEM((el, 4 * CAP, f), jnp.bfloat16),
            pltpu.VMEM((ring, f, cols), jnp.bfloat16),
            pltpu.VMEM((4, k3, cols), jnp.bfloat16),
            pltpu.VMEM((4, el * TAIL, cols), f32),
            pltpu.VMEM((2, 2, tok, cols), f32),
            pltpu.VMEM((chunks, 2, tok, cols), f32),
            pltpu.VMEM((tok, cols), f32),
            pltpu.VMEM((tok, cols), f32),
            pltpu.VMEM((chunks, tok, cols), f32),
            pltpu.VMEM((chunks, tok, cols), f32),
            pltpu.VMEM((2, tok, cols), f32),
            pltpu.VMEM((2, tok, cols), jnp.bfloat16),
            pltpu.SemaphoreType.DMA((4,)),
            pltpu.SemaphoreType.DMA((el,)),
            pltpu.SemaphoreType.DMA((ring,)),
            pltpu.SemaphoreType.DMA((chunks, 2)),
            pltpu.SemaphoreType.DMA((chunks, 2)),
            pltpu.SemaphoreType.DMA((chunks,)),
            pltpu.SemaphoreType.DMA((chunks,)),
            pltpu.SemaphoreType.DMA((2,)),
            pltpu.SemaphoreType.DMA((chunks,)),
            pltpu.SemaphoreType.DMA((chunks,)),
            pltpu.SemaphoreType.DMA((2,)),
        ],
        compiler_params=pltpu.CompilerParams(vmem_limit_bytes=63 * MIB, collective_id=0, has_side_effects=True),
        cost_estimate=pl.CostEstimate(flops=2 * el * 4 * CAP * f * d + 8 * tok * k3 * d,
                                      bytes_accessed=2 * el * f * d + 2 * el * 4 * CAP * f, transcendentals=0),
        name="route",
    )(g, h, w2, base, sy)


def solution(mesh):
    rows = P(("ep", "tp"), None)
    def body(x, idx, g, slot, ws1, ws3, ws2, w1, w3, w2):
        tok, d = x.shape
        el = w1.shape[0]
        kt = -(-el * CAP // 16) * 16
        code = jnp.where(slot >= 0, idx * 128 + slot, -1).astype(jnp.float32)
        mine = jnp.concatenate([code, g], axis=1).T
        cx, gm, base, sy, xc, xx, xxc = _front(x, mine, ws1, ws3, ws2, el, kt)
        h = _up((x, xc, xx, xxc), cx, w1, w3)
        return _route(gm, h, w2, base, sy)

    return jax.shard_map(
        body, mesh=mesh,
        in_specs=(rows, rows, rows, rows, P(None, "tp"), P(None, "tp"), P("tp", None),
                  P("ep", None, None), P("ep", None, None), P("ep", None, None)),
        out_specs=rows, check_vma=False)
```

profile of v0, /device:TPU:0, one launch (start us, length us, event | category | flops | bytes accessed | tf_op | source)
XLA Modules:
  0.0 270.0 jit_solution(1584642604843810637)
XLA Ops:
  0.0 0.7 select_convert_fusion
  0.7 1.3 maximum_bitcast_fusion.mine
  2.0 70.3 %front.1 = (f32[4,8,512]{2,1,0:T(8,128)}, bf16[2048,3264]{1,0:T(8,128)(2,1)}, f32[512,2048]{1,0:T(8,128)}, f32[512,2048]{1,0:T(8,128)}, bf16[512,2048]{1,0:T(8,1...) custom-call(bf16[512,2048]{1,0:T(8,128)(2,1)} %x0.1, f32[8,512]{1,0:T(8,128)} %maximum_bitcast_fusion.mine, ...), custom_call_target="tpu_custom_call" | custom-call | flops 35433480192 | bytes 34603008 | tf_op jit(solution)/shard_map/front/pallas_call | solution.py:177
  72.3 73.7 %up.1.h = bf16[15,288,1408]{2,1,0:T(8,128)(2,1)} custom-call(bf16[512,2048]{1,0:T(8,128)(2,1)} %x0.1, bf16[512,2048]{1,0:T(8,128)(2,1)} %get-tuple-element.13.x1, bf16[512,2048]{1,0:T(8,128)(2,1)} %get-tuple-element.14.x2, bf16[512,2048]{1,0:T(8,128)(2,1)} %get-tuple-element.15.x3, f32[4,8,512]{2,1,0:T(8,128)} %get-tuple-element.16.cx, ...), custom_call_target="tpu_custom_call" | custom-call | flops 49828331520 | bytes 173015040 | tf_op jit(solution)/shard_map/up/pallas_call | solution.py:273
  146.1 120.8 %route.1 = bf16[512,2048]{1,0:T(8,128)(2,1)} custom-call(bf16[2048,3264]{1,0:T(8,128)(2,1)} %get-tuple-element.12.g, bf16[15,288,1408]{2,1,0:T(8,128)(2,1)} %up.1.h, bf16[15,1408,2048]{2,1,0:T(8,128)(2,1)} %w2.3, f32[512,2048]{1,0:T(8,128)} %get-tuple-element.17.base, f32[512,2048]{1,0:T(8,128)} %get-tuple-element.18.sy), custom_call_target="tpu_custom_call" | custom-call | flops 52294582272 | bytes 98672640 | tf_op jit(solution)/shard_map/route/pallas_call | solution.py:457
  266.9 3.2 %copy.12 = bf16[512,2048]{1,0:T(8,128)(2,1)} copy(bf16[512,2048]{1,0:T(8,128)(2,1)} %route.1) | data formatting | bytes 4194304
where the time goes:
time: 270 us
  Pallas kernels  265 us (98%)
  local copies, waits for them, and re-layouts  3.16 us (1%)
    pallas_call x1, Pallas kernels, _route(): pl.pallas_call(functools.partial(_route_kernel, el, tok, cols), out_shape...  121 us
    pallas_call x1, Pallas kernels, _up(): pl.pallas_call(functools.partial(_up_kernel, el), grid=(el,), out_shape=j...  73.7 us
    pallas_call x1, Pallas kernels, _front(): pl.pallas_call(functools.partial(_front_kernel, el, kt), out_shape=[jax.S...  70.3 us

commit v1 on v0

--- a/solution.py
+++ b/solution.py
@@ -169,7 +169,7 @@
 def _front(x, mine, w1, w3, w2, el, kt):
     tok, d = x.shape
     f = w1.shape[1]
-    tf, tn = 256, 256
+    tf, tn = 256, 512
     nf, nn = f // tf, d // tn
     bf16, f32 = jnp.bfloat16, jnp.float32
     vmem = pl.BlockSpec(memory_space=pltpu.VMEM)
@@ -301,7 +301,6 @@
     kt = gv.shape[1] // 3
     nm = el * MAIN
     total = chunks * el
-    unroll = 5
 
     gcopy = lambda s: pltpu.make_async_copy(g.at[pl.ds(s * tok, tok)], gv.at[pl.ds(s * tok, tok)], gsem.at[s])
     hcopy = lambda e: pltpu.make_async_copy(h.at[e], hv.at[e], hsem.at[e])
@@ -344,30 +343,28 @@
     for c in range(2):
         bcopy(jnp.int32(c)).start()
 
-    def group(c, k):
-        for u in range(unroll):
-            t = c * el + k * unroll + u
-            wcopy(t).wait()
-
-            @pl.when(c == 0)
-            def _():
-                hcopy(k * unroll + u).wait()
-
-        for u in range(unroll):
-            e = k * unroll + u
+    def group(c, lo, hi):
+        for e in range(lo, hi):
+            wcopy(c * el + e).wait()
+
+        @pl.when(c == 0)
+        def _():
+            for e in range(lo, hi):
+                hcopy(e).wait()
+
+        for e in range(lo, hi):
             r = _dot(hv[e], wv[lax.rem(c * el + e, ring)]).astype(jnp.bfloat16)
-            row = pl.multiple_of(e * MAIN, MAIN)
             for s in range(4):
                 for i in range(3):
-                    r3[s, pl.ds(row + i * kt, MAIN), :] = r[s * MAIN:(s + 1) * MAIN]
+                    r3[s, e * MAIN + i * kt:(e + 1) * MAIN + i * kt, :] = r[s * MAIN:(s + 1) * MAIN]
             q = r[4 * MAIN:].astype(jnp.float32)
             for s in range(4):
-                rt[s, pl.ds(pl.multiple_of(e * TAIL, TAIL), TAIL), :] = q[s * TAIL:(s + 1) * TAIL]
-        for u in range(unroll):
-            t = c * el + k * unroll + u
+                rt[s, e * TAIL:(e + 1) * TAIL, :] = q[s * TAIL:(s + 1) * TAIL]
+        for e in range(lo, hi):
+            t = c * el + e
 
             @pl.when(t + ring < total)
-            def _():
+            def _(t=t):
                 wcopy(t + ring).start()
 
     def combine(s):
@@ -384,16 +381,13 @@
         across(c).start()
 
     def chunk(c, _):
-        def step(k, _):
-            group(c, k)
-
-            @pl.when((k == 0) & (c > 0))
-            def _():
-                merge(c - 1)
-
-            return 0
-
-        lax.fori_loop(0, el // unroll, step, 0)
+        group(c, 0, ring)
+
+        @pl.when(c > 0)
+        def _():
+            merge(c - 1)
+
+        group(c, ring, el)
 
         @pl.when(c == 0)
         def _():
@@ -409,8 +403,8 @@
         send[slot, 1] = combine(3)
         send[slot, 0] = combine(1)
         pair(c, 1).start()
+        pair(c, 0).start()
         far[...] = combine(2)
-        pair(c, 0).start()
         own[...] = combine(0)
         return 0
 

time: 270 us -> 262 us (0.970)
  Pallas kernels: 265 us -> 256 us
    pallas_call x1, Pallas kernels: 121 us -> 115 us  [_route(): pl.pallas_call(functools.partial(_route_kernel, el, tok, cols), out_shape...]
    pallas_call x1, Pallas kernels: 70.3 us -> 67.3 us  [_front(): pl.pallas_call(functools.partial(_front_kernel, el, kt), out_shape=[jax.S...]
where the time goes in v1:
time: 262 us; the launch traced here: 261 us
  Pallas kernels  256 us (98%)
  local copies, waits for them, and re-layouts  3.16 us (1%)
    pallas_call x1, Pallas kernels, _route(): pl.pallas_call(functools.partial(_route_kernel, el, tok, cols), out_shape...  115 us
    pallas_call x1, Pallas kernels, _up(): pl.pallas_call(functools.partial(_up_kernel, el), grid=(el,), out_shape=j...  73.7 us
    pallas_call x1, Pallas kernels, _front(): pl.pallas_call(functools.partial(_front_kernel, el, kt), out_shape=[jax.S...  67.3 us

profile of v1, /device:TPU:0, one launch (start us, length us, event | category | flops | bytes accessed | tf_op | source)
XLA Modules:
  0.0 261.3 jit_solution(4493642856652678144)
XLA Ops:
  0.0 0.7 select_convert_fusion
  0.7 1.3 maximum_bitcast_fusion.mine
  2.0 67.3 %front.1 = (f32[4,8,512]{2,1,0:T(8,128)}, bf16[2048,3264]{1,0:T(8,128)(2,1)}, f32[512,2048]{1,0:T(8,128)}, f32[512,2048]{1,0:T(8,128)}, bf16[512,2048]{1,0:T(8,1...) custom-call(bf16[512,2048]{1,0:T(8,128)(2,1)} %x0.1, f32[8,512]{1,0:T(8,128)} %maximum_bitcast_fusion.mine, ...), custom_call_target="tpu_custom_call" | custom-call | flops 35433480192 | bytes 34603008 | tf_op jit(solution)/shard_map/front/pallas_call | solution.py:177
  69.4 73.7 %up.1.h = bf16[15,288,1408]{2,1,0:T(8,128)(2,1)} custom-call(bf16[512,2048]{1,0:T(8,128)(2,1)} %x0.1, bf16[512,2048]{1,0:T(8,128)(2,1)} %get-tuple-element.13.x1, bf16[512,2048]{1,0:T(8,128)(2,1)} %get-tuple-element.14.x2, bf16[512,2048]{1,0:T(8,128)(2,1)} %get-tuple-element.15.x3, f32[4,8,512]{2,1,0:T(8,128)} %get-tuple-element.16.cx, ...), custom_call_target="tpu_custom_call" | custom-call | flops 49828331520 | bytes 173015040 | tf_op jit(solution)/shard_map/up/pallas_call | solution.py:273
  143.1 115.0 %route.1 = bf16[512,2048]{1,0:T(8,128)(2,1)} custom-call(bf16[2048,3264]{1,0:T(8,128)(2,1)} %get-tuple-element.12.g, bf16[15,288,1408]{2,1,0:T(8,128)(2,1)} %up.1.h, bf16[15,1408,2048]{2,1,0:T(8,128)(2,1)} %w2.3, f32[512,2048]{1,0:T(8,128)} %get-tuple-element.17.base, f32[512,2048]{1,0:T(8,128)} %get-tuple-element.18.sy), custom_call_target="tpu_custom_call" | custom-call | flops 52294582272 | bytes 98672640 | tf_op jit(solution)/shard_map/route/pallas_call | solution.py:451
  258.2 3.2 %copy.12 = bf16[512,2048]{1,0:T(8,128)(2,1)} copy(bf16[512,2048]{1,0:T(8,128)(2,1)} %route.1) | data formatting | bytes 4194304

commit v2 on v1

--- a/solution.py
+++ b/solution.py
@@ -24,10 +24,14 @@
 
 def _hot(c, n, base, tok):
     r = (lax.broadcasted_iota(jnp.int32, (n, tok), 0) + base).astype(jnp.float32)
-    hit = r == c[0:1, :]
-    for j in range(1, 4):
-        hit = hit | (r == c[j:j + 1, :])
-    return jnp.where(hit, 1.0, 0.0).astype(jnp.bfloat16)
+    g = jnp.zeros((n, tok), jnp.float32)
+    hit = None
+    for j in range(4):
+        same = r == c[j:j + 1, :]
+        hit = same if hit is None else hit | same
+        g = jnp.where(same, c[4 + j:5 + j, :], g)
+    g = jnp.broadcast_to(jnp.sum(g, axis=1, keepdims=True), (n, 128))
+    return jnp.where(hit, 1.0, 0.0).astype(jnp.bfloat16), g
 
 
 def _codes(t, me, el):
@@ -36,10 +40,7 @@
     le = e - me * el
     ok = (code >= 0) & (le >= 0) & (le < el)
     c = jnp.where(ok, jnp.where(k < MAIN, le * MAIN + k, el * MAIN + le * TAIL + k - MAIN), -1).astype(jnp.float32)
-    g = t[4:8, :]
-    g0 = g.astype(jnp.bfloat16).astype(jnp.float32)
-    g1 = (g - g0).astype(jnp.bfloat16).astype(jnp.float32)
-    return c, jnp.concatenate([c, g0, g1, g - g0 - g1], axis=0)
+    return c
 
 
 def _front_kernel(el, kt, x, mine, w1, w3, w2, cx, gm, base, sy, xc, xx, xxc,
@@ -85,10 +86,13 @@
     for i in range(nn):
         down(i).start()
 
-    def store_tab(s, tab):
-        wide = jnp.concatenate([tab, jnp.zeros((128 - tab.shape[0], tok), jnp.float32)], axis=0)
+    def table(k):
+        t = mine[...] if k == 0 else tabs[k - 1]
+        c = _codes(t, me, el)
+        cx[k] = jnp.concatenate([c, t[4:8, :]], axis=0)
+        wide = jnp.concatenate([c, jnp.zeros((124, tok), jnp.float32)], axis=0)
         for b in range(0, tok, 128):
-            tabt[s * tok + b:s * tok + b + 128, :] = jnp.transpose(wide[:, b:b + 128])
+            tabt[k * tok + b:k * tok + b + 128, :] = jnp.transpose(wide[:, b:b + 128])
 
     def shared(src, lo, n, out, add, first):
         scopy = lambda i: pltpu.make_async_copy(
@@ -124,38 +128,33 @@
         for i in (nn - 2, nn - 1):
             scopy(jnp.int32(i)).wait()
 
-    shared(x, 0, tok, base, True, True)
-    for k in range(4):
-        if k:
-            tcopy[k - 1].wait()
-        c, tab = _codes(mine[...] if k == 0 else tabs[k - 1], me, el)
-        cx[k] = jnp.concatenate([c, c], axis=0)
-        store_tab(k, tab)
-
     blk = gst.shape[1]
     gcopy = lambda i: pltpu.make_async_copy(gst.at[lax.rem(i, 2)], gm.at[pl.ds(pl.multiple_of(i * blk, blk), blk)], gsem.at[lax.rem(i, 2)])
 
-    def gates(i, _):
+    def picks(i, _):
         @pl.when(i >= 2)
         def _():
             gcopy(i - 2).wait()
 
         t = tabt[pl.ds(pl.multiple_of(i * blk, blk), blk), :]
         lane = lax.broadcasted_iota(jnp.int32, (blk, kt), 1).astype(jnp.float32)
-        acc = [jnp.zeros((blk, kt), jnp.float32) for _ in range(3)]
-        for j in range(4):
-            hit = t[:, j:j + 1] == lane
-            for q in range(3):
-                acc[q] = jnp.where(hit, t[:, 4 + 4 * q + j:5 + 4 * q + j], acc[q])
-        for q in range(3):
-            gst[lax.rem(i, 2), :, q * kt:(q + 1) * kt] = acc[q].astype(jnp.bfloat16)
+        hit = t[:, 0:1] == lane
+        for j in range(1, 4):
+            hit = hit | (t[:, j:j + 1] == lane)
+        gst[lax.rem(i, 2)] = jnp.where(hit, 1.0, 0.0).astype(jnp.bfloat16)
         gcopy(i).start()
         return 0
 
-    ng = 4 * tok // blk
-    lax.fori_loop(0, ng, gates, 0)
-    for i in (ng - 2, ng - 1):
+    ng = tok // blk
+    table(0)
+    lax.fori_loop(0, ng, picks, 0)
+    for k in range(1, 4):
+        tcopy[k - 1].wait()
+        table(k)
+    lax.fori_loop(ng, 4 * ng, picks, 0)
+    for i in (4 * ng - 2, 4 * ng - 1):
         gcopy(jnp.int32(i)).wait()
+    shared(x, 0, tok, base, True, True)
     ycopy[0].wait()
     shared(y, 0, half, sy, False, False)
     xcopy.wait()
@@ -177,7 +176,7 @@
     return pl.pallas_call(
         functools.partial(_front_kernel, el, kt),
         out_shape=[jax.ShapeDtypeStruct(sh, dt) for sh, dt in (
-            ((4, 8, tok), f32), ((4 * tok, 3 * kt), bf16), ((tok, d), f32), ((tok, d), f32),
+            ((4, 8, tok), f32), ((4 * tok, kt), bf16), ((tok, d), f32), ((tok, d), f32),
             ((tok, d), bf16), ((tok, d), bf16), ((tok, d), bf16))],
         in_specs=[vmem, vmem] + [ANY] * 3,
         out_specs=[vmem] + [ANY] * 6,
@@ -190,7 +189,7 @@
             pltpu.VMEM((nn, f, tn), bf16),
             pltpu.VMEM((tok, f), bf16),
             pltpu.VMEM((2, tok, tn), f32),
-            pltpu.VMEM((2, 128, 3 * kt), bf16),
+            pltpu.VMEM((2, 128, kt), bf16),
             dma((2 * nf + nn,)), dma((5,)), dma((5,)), dma((3,)), dma((3,)), dma((2,)), dma((2,)),
         ],
         compiler_params=pltpu.CompilerParams(vmem_limit_bytes=62 * MIB, collective_id=1, has_side_effects=True),
@@ -199,7 +198,7 @@
     )(x, mine, w1, w3, w2)
 
 
-def _up_kernel(el, x0, x1, x2, x3, cx, w1, w3, h, xs, tg, xb, wv, xsem, wsem):
+def _up_kernel(el, x0, x1, x2, x3, cx, w1, w3, h, gs, xs, tg, xb, wv, xsem, wsem):
     e = pl.program_id(0)
     tok, d = x0.shape
     ring = wv.shape[0]
@@ -224,12 +223,16 @@
             xcopy(0, k).wait()
             c = cx[s]
             for b in range(0, el, some):
-                p = _hot(c, some * MAIN, b * MAIN, tok)
+                p, g = _hot(c, some * MAIN, b * MAIN, tok)
+                for i in range(some):
+                    gs[b + i, pl.ds(pl.multiple_of(s * MAIN, MAIN), MAIN), :] = g[i * MAIN:(i + 1) * MAIN]
                 for n in range(0, d, 512):
                     r = _dot(p, xb[k, :, n:n + 512]).astype(jnp.bfloat16)
                     for i in range(some):
                         xs[b + i, pl.ds(pl.multiple_of(s * MAIN, MAIN), MAIN), n:n + 512] = r[i * MAIN:(i + 1) * MAIN]
-            p = _hot(c, el * TAIL, el * MAIN, tok)
+            p, g = _hot(c, el * TAIL, el * MAIN, tok)
+            for i in range(el):
+                gs[i, pl.ds(pl.multiple_of(4 * MAIN + s * TAIL, TAIL), TAIL), :] = g[i * TAIL:(i + 1) * TAIL]
             for n in range(0, d, 512):
                 tg[s, :, n:n + 512] = _dot(p, xb[k, :, n:n + 512])
             for j in range(2):
@@ -273,9 +276,9 @@
     return pl.pallas_call(
         functools.partial(_up_kernel, el),
         grid=(el,),
-        out_shape=jax.ShapeDtypeStruct((el, 4 * CAP, f), jnp.bfloat16),
+        out_shape=[jax.ShapeDtypeStruct((el, 4 * CAP, f), jnp.bfloat16), jax.ShapeDtypeStruct((el, 4 * CAP, 128), jnp.float32)],
         in_specs=[ANY] * 4 + [pl.BlockSpec(cx.shape, lambda e: (0, 0, 0))] + [ANY] * 2,
-        out_specs=pl.BlockSpec((1, 4 * CAP, f), lambda e: (e, 0, 0)),
+        out_specs=[pl.BlockSpec((1, 4 * CAP, f), lambda e: (e, 0, 0)), pl.BlockSpec((el, 4 * CAP, 128), lambda e: (0, 0, 0))],
         scratch_shapes=[
             pltpu.VMEM((el, 4 * CAP, d), jnp.bfloat16),
             pltpu.VMEM((4, el * TAIL, d), jnp.float32),
@@ -290,7 +293,7 @@
     )(*xs, cx, w1, w3)
 
 
-def _route_kernel(el, tok, cols, g, h, w2, base, sy, out, gv, hv, wv, r3, rt, send, recv, far, own, back, yb, bv, ost,
+def _route_kernel(el, tok, cols, g, gs, h, w2, base, sy, out, gv, gsv, hv, wv, r3, rt, send, recv, far, own, back, yb, bv, ost,
                   gsem, hsem, wsem, ssem, rsem, xssem, xrsem, osem, yssem, yrsem, bsem):
     me = lax.axis_index("ep")
     tp = lax.axis_index("tp")
@@ -298,12 +301,19 @@
     peer = lax.rem(me + 2, 4)
     ring = wv.shape[0]
     chunks = back.shape[0]
-    kt = gv.shape[1] // 3
+    kt = gv.shape[1]
     nm = el * MAIN
     total = chunks * el
 
     gcopy = lambda s: pltpu.make_async_copy(g.at[pl.ds(s * tok, tok)], gv.at[pl.ds(s * tok, tok)], gsem.at[s])
     hcopy = lambda e: pltpu.make_async_copy(h.at[e], hv.at[e], hsem.at[e])
+    gscopy = pltpu.make_async_copy(gs, gsv, gsem.at[4])
+
+    def split(v):
+        hi = v.astype(jnp.bfloat16)
+        v = v - hi.astype(jnp.float32)
+        mid = v.astype(jnp.bfloat16)
+        return hi, mid, (v - mid.astype(jnp.float32)).astype(jnp.bfloat16)
 
     def wcopy(t):
         slot = lax.rem(t, ring)
@@ -327,6 +337,7 @@
     bcopy = lambda c: pltpu.make_async_copy(part(base, c), bv.at[lax.rem(c, 2)], bsem.at[lax.rem(c, 2)])
     ocopy = lambda c: pltpu.make_async_copy(ost.at[lax.rem(c, 2)], part(out, c), osem.at[lax.rem(c, 2)])
 
+    gscopy.start()
     for e in range(el):
         hcopy(e).start()
         if e < ring:
@@ -349,17 +360,18 @@
 
         @pl.when(c == 0)
         def _():
+            if lo == 0:
+                gscopy.wait()
             for e in range(lo, hi):
                 hcopy(e).wait()
 
         for e in range(lo, hi):
-            r = _dot(hv[e], wv[lax.rem(c * el + e, ring)]).astype(jnp.bfloat16)
+            r = _dot(hv[e], wv[lax.rem(c * el + e, ring)]).astype(jnp.bfloat16).astype(jnp.float32)
+            r = r * jnp.concatenate([gsv[e]] * (cols // 128), axis=1)
             for s in range(4):
-                for i in range(3):
-                    r3[s, e * MAIN + i * kt:(e + 1) * MAIN + i * kt, :] = r[s * MAIN:(s + 1) * MAIN]
-            q = r[4 * MAIN:].astype(jnp.float32)
-            for s in range(4):
-                rt[s, e * TAIL:(e + 1) * TAIL, :] = q[s * TAIL:(s + 1) * TAIL]
+                for i, v in enumerate(split(r[s * MAIN:(s + 1) * MAIN])):
+                    r3[s, e * MAIN + i * kt:(e + 1) * MAIN + i * kt, :] = v
+                rt[s, e * TAIL:(e + 1) * TAIL, :] = r[4 * MAIN + s * TAIL:4 * MAIN + (s + 1) * TAIL]
         for e in range(lo, hi):
             t = c * el + e
 
@@ -368,10 +380,11 @@
                 wcopy(t + ring).start()
 
     def combine(s):
-        tail = jnp.concatenate([rt[s], jnp.zeros((kt - el * CAP, cols), jnp.float32)], axis=0).astype(jnp.bfloat16)
-        for i in range(3):
-            r3[s, i * kt + nm:(i + 1) * kt, :] = tail
-        return _dot(gv[s * tok:(s + 1) * tok, :], r3[s])
+        tail = jnp.concatenate([rt[s], jnp.zeros((kt - el * CAP, cols), jnp.float32)], axis=0)
+        for i, v in enumerate(split(tail)):
+            r3[s, i * kt + nm:(i + 1) * kt, :] = v
+        p = gv[s * tok:(s + 1) * tok, :]
+        return sum(_dot(p, r3[s, i * kt:(i + 1) * kt, :]) for i in range(1, 3)) + _dot(p, r3[s, 0:kt, :])
 
     def merge(c):
         pair(c, 1).wait_recv()
@@ -383,7 +396,7 @@
     def chunk(c, _):
         group(c, 0, ring)
 
-        @pl.when(c > 0)
+        @pl.when(c > 1)
         def _():
             merge(c - 1)
 
@@ -406,6 +419,11 @@
         pair(c, 0).start()
         far[...] = combine(2)
         own[...] = combine(0)
+
+        @pl.when(c == 0)
+        def _():
+            merge(c)
+
         return 0
 
     lax.fori_loop(0, chunks, chunk, 0)
@@ -440,24 +458,25 @@
         ycopy(jnp.int32(c)).wait_send()
 
 
-def _route(g, h, w2, base, sy):
+def _route(g, gs, h, w2, base, sy):
     el, f, d = w2.shape
     tok = base.shape[0]
     cols = 256
     chunks = d // cols
     ring = 8
-    k3 = g.shape[1]
+    kt = g.shape[1]
     f32 = jnp.float32
     return pl.pallas_call(
         functools.partial(_route_kernel, el, tok, cols),
         out_shape=jax.ShapeDtypeStruct((tok, d), jnp.bfloat16),
-        in_specs=[ANY] * 5,
+        in_specs=[ANY] * 6,
         out_specs=ANY,
         scratch_shapes=[
-            pltpu.VMEM((4 * tok, k3), jnp.bfloat16),
+            pltpu.VMEM((4 * tok, kt), jnp.bfloat16),
+            pltpu.VMEM(gs.shape, f32),
             pltpu.VMEM((el, 4 * CAP, f), jnp.bfloat16),
             pltpu.VMEM((ring, f, cols), jnp.bfloat16),
-            pltpu.VMEM((4, k3, cols), jnp.bfloat16),
+            pltpu.VMEM((4, 3 * kt, cols), jnp.bfloat16),
             pltpu.VMEM((4, el * TAIL, cols), f32),
             pltpu.VMEM((2, 2, tok, cols), f32),
             pltpu.VMEM((chunks, 2, tok, cols), f32),
@@ -467,7 +486,7 @@
             pltpu.VMEM((chunks, tok, cols), f32),
             pltpu.VMEM((2, tok, cols), f32),
             pltpu.VMEM((2, tok, cols), jnp.bfloat16),
-            pltpu.SemaphoreType.DMA((4,)),
+            pltpu.SemaphoreType.DMA((5,)),
             pltpu.SemaphoreType.DMA((el,)),
             pltpu.SemaphoreType.DMA((ring,)),
             pltpu.SemaphoreType.DMA((chunks, 2)),
@@ -480,10 +499,10 @@
             pltpu.SemaphoreType.DMA((2,)),
         ],
         compiler_params=pltpu.CompilerParams(vmem_limit_bytes=63 * MIB, collective_id=0, has_side_effects=True),
-        cost_estimate=pl.CostEstimate(flops=2 * el * 4 * CAP * f * d + 8 * tok * k3 * d,
+        cost_estimate=pl.CostEstimate(flops=2 * el * 4 * CAP * f * d + 24 * tok * kt * d,
                                       bytes_accessed=2 * el * f * d + 2 * el * 4 * CAP * f, transcendentals=0),
         name="route",
-    )(g, h, w2, base, sy)
+    )(g, gs, h, w2, base, sy)
 
 
 def solution(mesh):
@@ -495,8 +514,8 @@
         code = jnp.where(slot >= 0, idx * 128 + slot, -1).astype(jnp.float32)
         mine = jnp.concatenate([code, g], axis=1).T
         cx, gm, base, sy, xc, xx, xxc = _front(x, mine, ws1, ws3, ws2, el, kt)
-        h = _up((x, xc, xx, xxc), cx, w1, w3)
-        return _route(gm, h, w2, base, sy)
+        h, gs = _up((x, xc, xx, xxc), cx, w1, w3)
+        return _route(gm, gs, h, w2, base, sy)
 
     return jax.shard_map(
         body, mesh=mesh,

time: 262 us -> 263 us (level)
  no operation moved by 1% of the time
where the time goes in v2:
time: 263 us; the launch traced here: 262 us
  Pallas kernels  257 us (98%)
  local copies, waits for them, and re-layouts  3.16 us (1%)
    pallas_call x1, Pallas kernels, _route(): pl.pallas_call(functools.partial(_route_kernel, el, tok, cols), out_shape...  115 us
    pallas_call x1, Pallas kernels, _up(): pl.pallas_call(functools.partial(_up_kernel, el), grid=(el,), out_shape=[...  76 us
    pallas_call x1, Pallas kernels, _front(): pl.pallas_call(functools.partial(_front_kernel, el, kt), out_shape=[jax.S...  66 us

profile of v2, /device:TPU:0, one launch (start us, length us, event | category | flops | bytes accessed | tf_op | source)
XLA Modules:
  0.0 262.4 jit_solution(9365054217595059001)
XLA Ops:
  0.0 0.7 select_convert_fusion
  0.7 1.3 maximum_bitcast_fusion.mine
  2.0 66.0 %front.1 = (f32[4,8,512]{2,1,0:T(8,128)}, bf16[2048,1088]{1,0:T(8,128)(2,1)}, f32[512,2048]{1,0:T(8,128)}, f32[512,2048]{1,0:T(8,128)}, bf16[512,2048]{1,0:T(8,1...) custom-call(bf16[512,2048]{1,0:T(8,128)(2,1)} %x0.1, f32[8,512]{1,0:T(8,128)} %maximum_bitcast_fusion.mine, ...), custom_call_target="tpu_custom_call" | custom-call | flops 35433480192 | bytes 34603008 | tf_op jit(solution)/shard_map/front/pallas_call | solution.py:176
  68.0 76.0 %up.1 = (bf16[15,288,1408]{2,1,0:T(8,128)(2,1)}, f32[15,288,128]{2,1,0:T(8,128)}) custom-call(bf16[512,2048]{1,0:T(8,128)(2,1)} %x0.1, bf16[512,2048]{1,0:T(8,128)(2,1)} %get-tuple-element.15.x1, bf16[512,2048]{1,0:T(8,128)(2,1)} %get-tuple-element.16.x2, bf16[512,2048]{1,0:T(8,128)(2,1)} %get-tuple-element.17.x3, f32[4,8,512]{2,1,0:T(8,128)} %get-tuple-element.18.cx, ...), custom_call_target="tpu_custom_call" | custom-call | flops 49828331520 | bytes 173015040 | tf_op jit(solution)/shard_map/up/pallas_call | solution.py:276
  144.0 115.3 %route.1 = bf16[512,2048]{1,0:T(8,128)(2,1)} custom-call(bf16[2048,1088]{1,0:T(8,128)(2,1)} %get-tuple-element.14.g, f32[15,288,128]{2,1,0:T(8,128)} %get-tuple-element.19.gs, bf16[15,288,1408]{2,1,0:T(8,128)(2,1)} %get-tuple-element.20.h, bf16[15,1408,2048]{2,1,0:T(8,128)(2,1)} %w2.3, f32[512,2048]{1,0:T(8,128)} %get-tuple-element.21.base, ...), custom_call_target="tpu_custom_call" | custom-call | flops 52294582272 | bytes 98672640 | tf_op jit(solution)/shard_map/route/pallas_call | solution.py:469
  259.3 3.2 %copy.12 = bf16[512,2048]{1,0:T(8,128)(2,1)} copy(bf16[512,2048]{1,0:T(8,128)(2,1)} %route.1) | data formatting | bytes 4194304

commit v3 on v2

--- a/solution.py
+++ b/solution.py
@@ -25,13 +25,10 @@
 def _hot(c, n, base, tok):
     r = (lax.broadcasted_iota(jnp.int32, (n, tok), 0) + base).astype(jnp.float32)
     g = jnp.zeros((n, tok), jnp.float32)
-    hit = None
     for j in range(4):
-        same = r == c[j:j + 1, :]
-        hit = same if hit is None else hit | same
-        g = jnp.where(same, c[4 + j:5 + j, :], g)
-    g = jnp.broadcast_to(jnp.sum(g, axis=1, keepdims=True), (n, 128))
-    return jnp.where(hit, 1.0, 0.0).astype(jnp.bfloat16), g
+        g = jnp.where(r == c[j:j + 1, :], c[4 + j:5 + j, :], g)
+    pick = jnp.where(g > 0, 1.0, 0.0).astype(jnp.bfloat16)
+    return pick, jnp.broadcast_to(jnp.sum(g, axis=1, keepdims=True), (n, 128))
 
 
 def _codes(t, me, el):
@@ -337,13 +334,11 @@
     bcopy = lambda c: pltpu.make_async_copy(part(base, c), bv.at[lax.rem(c, 2)], bsem.at[lax.rem(c, 2)])
     ocopy = lambda c: pltpu.make_async_copy(ost.at[lax.rem(c, 2)], part(out, c), osem.at[lax.rem(c, 2)])
 
+    first = (el + 1) // 2
     gscopy.start()
-    for e in range(el):
+    for e in range(first):
         hcopy(e).start()
-        if e < ring:
-            wcopy(jnp.int32(e)).start()
-    for s in (3, 1, 2, 0):
-        gcopy(s).start()
+        wcopy(jnp.int32(e)).start()
     barrier = pltpu.get_barrier_semaphore()
     for dev in (sib, peer):
         pl.semaphore_signal(barrier, inc=1, device_id={"ep": dev}, device_id_type=pl.DeviceIdType.MESH)
@@ -351,8 +346,6 @@
     pl.semaphore_wait(barrier, 3)
     for c in range(chunks):
         ycopy(jnp.int32(c)).start()
-    for c in range(2):
-        bcopy(jnp.int32(c)).start()
 
     def group(c, lo, hi):
         for e in range(lo, hi):
@@ -364,6 +357,15 @@
                 gscopy.wait()
             for e in range(lo, hi):
                 hcopy(e).wait()
+            if lo == 0:
+                for e in range(hi, el):
+                    hcopy(e).start()
+                    wcopy(jnp.int32(e)).start()
+            else:
+                for s in (3, 1, 2, 0):
+                    gcopy(s).start()
+                for b in range(2):
+                    bcopy(jnp.int32(b)).start()
 
         for e in range(lo, hi):
             r = _dot(hv[e], wv[lax.rem(c * el + e, ring)]).astype(jnp.bfloat16).astype(jnp.float32)
@@ -394,13 +396,13 @@
         across(c).start()
 
     def chunk(c, _):
-        group(c, 0, ring)
+        group(c, 0, first)
 
         @pl.when(c > 1)
         def _():
             merge(c - 1)
 
-        group(c, ring, el)
+        group(c, first, el)
 
         @pl.when(c == 0)
         def _():
@@ -463,7 +465,7 @@
     tok = base.shape[0]
     cols = 256
     chunks = d // cols
-    ring = 8
+    ring = el
     kt = g.shape[1]
     f32 = jnp.float32
     return pl.pallas_call(

time: 263 us -> 258 us (0.981)
  Pallas kernels: 257 us -> 253 us
    pallas_call x1, Pallas kernels: 76 us -> 72.9 us  [_up(): pl.pallas_call(functools.partial(_up_kernel, el), grid=(el,), out_shape=[...]
where the time goes in v3:
time: 258 us
  Pallas kernels  253 us (98%)
  local copies, waits for them, and re-layouts  3.16 us (1%)
    pallas_call x1, Pallas kernels, _route(): pl.pallas_call(functools.partial(_route_kernel, el, tok, cols), out_shape...  114 us
    pallas_call x1, Pallas kernels, _up(): pl.pallas_call(functools.partial(_up_kernel, el), grid=(el,), out_shape=[...  72.9 us
    pallas_call x1, Pallas kernels, _front(): pl.pallas_call(functools.partial(_front_kernel, el, kt), out_shape=[jax.S...  66 us

profile of v3, /device:TPU:0, one launch (start us, length us, event | category | flops | bytes accessed | tf_op | source)
XLA Modules:
  0.0 258.1 jit_solution(4488318943132476116)
XLA Ops:
  0.0 0.7 select_convert_fusion
  0.7 1.3 maximum_bitcast_fusion.mine
  2.0 66.0 %front.1 = (f32[4,8,512]{2,1,0:T(8,128)}, bf16[2048,1088]{1,0:T(8,128)(2,1)}, f32[512,2048]{1,0:T(8,128)}, f32[512,2048]{1,0:T(8,128)}, bf16[512,2048]{1,0:T(8,1...) custom-call(bf16[512,2048]{1,0:T(8,128)(2,1)} %x0.1, f32[8,512]{1,0:T(8,128)} %maximum_bitcast_fusion.mine, ...), custom_call_target="tpu_custom_call" | custom-call | flops 35433480192 | bytes 34603008 | tf_op jit(solution)/shard_map/front/pallas_call | solution.py:173
  68.0 72.9 %up.1 = (bf16[15,288,1408]{2,1,0:T(8,128)(2,1)}, f32[15,288,128]{2,1,0:T(8,128)}) custom-call(bf16[512,2048]{1,0:T(8,128)(2,1)} %x0.1, bf16[512,2048]{1,0:T(8,128)(2,1)} %get-tuple-element.15.x1, bf16[512,2048]{1,0:T(8,128)(2,1)} %get-tuple-element.16.x2, bf16[512,2048]{1,0:T(8,128)(2,1)} %get-tuple-element.17.x3, f32[4,8,512]{2,1,0:T(8,128)} %get-tuple-element.18.cx, ...), custom_call_target="tpu_custom_call" | custom-call | flops 49828331520 | bytes 173015040 | tf_op jit(solution)/shard_map/up/pallas_call | solution.py:273
  140.9 114.1 %route.1 = bf16[512,2048]{1,0:T(8,128)(2,1)} custom-call(bf16[2048,1088]{1,0:T(8,128)(2,1)} %get-tuple-element.14.g, f32[15,288,128]{2,1,0:T(8,128)} %get-tuple-element.19.gs, bf16[15,288,1408]{2,1,0:T(8,128)(2,1)} %get-tuple-element.20.h, bf16[15,1408,2048]{2,1,0:T(8,128)(2,1)} %w2.3, f32[512,2048]{1,0:T(8,128)} %get-tuple-element.21.base, ...), custom_call_target="tpu_custom_call" | custom-call | flops 52294582272 | bytes 98672640 | tf_op jit(solution)/shard_map/route/pallas_call | solution.py:471
  254.9 3.2 %copy.12 = bf16[512,2048]{1,0:T(8,128)(2,1)} copy(bf16[512,2048]{1,0:T(8,128)(2,1)} %route.1) | data formatting | bytes 4194304

commit v4 on v3

--- a/solution.py
+++ b/solution.py
@@ -48,7 +48,7 @@
     peer = lax.rem(me + 2, 4)
     diag = lax.rem(sib + 2, 4)
     tok, d = x.shape
-    half = tok // 2
+    parts = ((0, tok * 5 // 8), (tok * 5 // 8, tok * 3 // 8))
     nf, nn = v1.shape[0], v2.shape[0]
     tf, tn = v1.shape[2], v2.shape[2]
     mesh_id = pl.DeviceIdType.MESH
@@ -72,8 +72,8 @@
     tcopy = [remote(mine, tabs.at[k], tsend.at[k], trecv.at[k], {"ep": dev}) for k, dev in enumerate((sib, peer, diag))]
     xcopy = remote(x, xx, xsend.at[0], xrecv.at[0], {"ep": peer})
     ccopy = remote(x, xc, xsend.at[1], xrecv.at[1], {"ep": sib})
-    ycopy = [remote(x.at[pl.ds(k * half, half)], y.at[pl.ds(k * half, half)], xsend.at[2 + k], xrecv.at[2 + k], {"tp": 1 - tp})
-             for k in range(2)]
+    ycopy = [remote(x.at[pl.ds(*r)], y.at[pl.ds(*r)], xsend.at[2 + k], xrecv.at[2 + k], {"tp": 1 - tp})
+             for k, r in enumerate(parts)]
     relay = remote(xx, xxc, xsend.at[4], xrecv.at[4], {"ep": sib})
     for c in (*tcopy, xcopy, *ycopy, ccopy):
         c.start()
@@ -153,11 +153,11 @@
         gcopy(jnp.int32(i)).wait()
     shared(x, 0, tok, base, True, True)
     ycopy[0].wait()
-    shared(y, 0, half, sy, False, False)
+    shared(y, *parts[0], sy, False, False)
     xcopy.wait()
     relay.start()
     ycopy[1].wait()
-    shared(y, half, half, sy, False, False)
+    shared(y, *parts[1], sy, False, False)
     ccopy.wait()
     relay.wait()
 
@@ -344,8 +344,6 @@
         pl.semaphore_signal(barrier, inc=1, device_id={"ep": dev}, device_id_type=pl.DeviceIdType.MESH)
     pl.semaphore_signal(barrier, inc=1, device_id={"tp": 1 - tp}, device_id_type=pl.DeviceIdType.MESH)
     pl.semaphore_wait(barrier, 3)
-    for c in range(chunks):
-        ycopy(jnp.int32(c)).start()
 
     def group(c, lo, hi):
         for e in range(lo, hi):
@@ -397,6 +395,7 @@
 
     def chunk(c, _):
         group(c, 0, first)
+        ycopy(c).start()
 
         @pl.when(c > 1)
         def _():

time: 258 us -> 256 us (level)
  no operation moved by 1% of the time
where the time goes in v4:
time: 256 us
  Pallas kernels  251 us (98%)
  local copies, waits for them, and re-layouts  3.16 us (1%)
    pallas_call x1, Pallas kernels, _route(): pl.pallas_call(functools.partial(_route_kernel, el, tok, cols), out_shape...  114 us
    pallas_call x1, Pallas kernels, _up(): pl.pallas_call(functools.partial(_up_kernel, el), grid=(el,), out_shape=[...  72.9 us
    pallas_call x1, Pallas kernels, _front(): pl.pallas_call(functools.partial(_front_kernel, el, kt), out_shape=[jax.S...  63.8 us

profile of v4, /device:TPU:0, one launch (start us, length us, event | category | flops | bytes accessed | tf_op | source)
XLA Modules:
  0.0 256.0 jit_solution(15062219831679255888)
XLA Ops:
  0.0 0.7 select_convert_fusion
  0.7 1.3 maximum_bitcast_fusion.mine
  2.0 63.8 %front.1 = (f32[4,8,512]{2,1,0:T(8,128)}, bf16[2048,1088]{1,0:T(8,128)(2,1)}, f32[512,2048]{1,0:T(8,128)}, f32[512,2048]{1,0:T(8,128)}, bf16[512,2048]{1,0:T(8,1...) custom-call(bf16[512,2048]{1,0:T(8,128)(2,1)} %x0.1, f32[8,512]{1,0:T(8,128)} %maximum_bitcast_fusion.mine, ...), custom_call_target="tpu_custom_call" | custom-call | flops 35433480192 | bytes 34603008 | tf_op jit(solution)/shard_map/front/pallas_call | solution.py:173
  65.9 72.9 %up.1 = (bf16[15,288,1408]{2,1,0:T(8,128)(2,1)}, f32[15,288,128]{2,1,0:T(8,128)}) custom-call(bf16[512,2048]{1,0:T(8,128)(2,1)} %x0.1, bf16[512,2048]{1,0:T(8,128)(2,1)} %get-tuple-element.15.x1, bf16[512,2048]{1,0:T(8,128)(2,1)} %get-tuple-element.16.x2, bf16[512,2048]{1,0:T(8,128)(2,1)} %get-tuple-element.17.x3, f32[4,8,512]{2,1,0:T(8,128)} %get-tuple-element.18.cx, ...), custom_call_target="tpu_custom_call" | custom-call | flops 49828331520 | bytes 173015040 | tf_op jit(solution)/shard_map/up/pallas_call | solution.py:273
  138.8 114.0 %route.1 = bf16[512,2048]{1,0:T(8,128)(2,1)} custom-call(bf16[2048,1088]{1,0:T(8,128)(2,1)} %get-tuple-element.14.g, f32[15,288,128]{2,1,0:T(8,128)} %get-tuple-element.19.gs, bf16[15,288,1408]{2,1,0:T(8,128)(2,1)} %get-tuple-element.20.h, bf16[15,1408,2048]{2,1,0:T(8,128)(2,1)} %w2.3, f32[512,2048]{1,0:T(8,128)} %get-tuple-element.21.base, ...), custom_call_target="tpu_custom_call" | custom-call | flops 52294582272 | bytes 98672640 | tf_op jit(solution)/shard_map/route/pallas_call | solution.py:470
  252.8 3.2 %copy.12 = bf16[512,2048]{1,0:T(8,128)(2,1)} copy(bf16[512,2048]{1,0:T(8,128)(2,1)} %route.1) | data formatting | bytes 4194304

commit v5 on v4

--- a/solution.py
+++ b/solution.py
@@ -334,11 +334,17 @@
     bcopy = lambda c: pltpu.make_async_copy(part(base, c), bv.at[lax.rem(c, 2)], bsem.at[lax.rem(c, 2)])
     ocopy = lambda c: pltpu.make_async_copy(ost.at[lax.rem(c, 2)], part(out, c), osem.at[lax.rem(c, 2)])
 
-    first = (el + 1) // 2
+    size = 4
+    blocks = [(lo, min(lo + size, el)) for lo in range(0, el, size)]
+
+    def load(k):
+        for e in range(*blocks[k]):
+            hcopy(e).start()
+            wcopy(jnp.int32(e)).start()
+
+    load(0)
     gscopy.start()
-    for e in range(first):
-        hcopy(e).start()
-        wcopy(jnp.int32(e)).start()
+    load(1)
     barrier = pltpu.get_barrier_semaphore()
     for dev in (sib, peer):
         pl.semaphore_signal(barrier, inc=1, device_id={"ep": dev}, device_id_type=pl.DeviceIdType.MESH)
@@ -355,11 +361,9 @@
                 gscopy.wait()
             for e in range(lo, hi):
                 hcopy(e).wait()
-            if lo == 0:
-                for e in range(hi, el):
-                    hcopy(e).start()
-                    wcopy(jnp.int32(e)).start()
-            else:
+            if lo + 2 * size < el:
+                load(lo // size + 2)
+            elif hi < el:
                 for s in (3, 1, 2, 0):
                     gcopy(s).start()
                 for b in range(2):
@@ -394,14 +398,15 @@
         across(c).start()
 
     def chunk(c, _):
-        group(c, 0, first)
+        group(c, *blocks[0])
         ycopy(c).start()
 
         @pl.when(c > 1)
         def _():
             merge(c - 1)
 
-        group(c, first, el)
+        for b in blocks[1:]:
+            group(c, *b)
 
         @pl.when(c == 0)
         def _():

time: 256 us -> 254 us (level)
  no operation moved by 1% of the time
where the time goes in v5:
time: 254 us
  Pallas kernels  249 us (98%)
  local copies, waits for them, and re-layouts  3.16 us (1%)
    pallas_call x1, Pallas kernels, _route(): pl.pallas_call(functools.partial(_route_kernel, el, tok, cols), out_shape...  112 us
    pallas_call x1, Pallas kernels, _up(): pl.pallas_call(functools.partial(_up_kernel, el), grid=(el,), out_shape=[...  72.9 us
    pallas_call x1, Pallas kernels, _front(): pl.pallas_call(functools.partial(_front_kernel, el, kt), out_shape=[jax.S...  63.8 us

profile of v5, /device:TPU:0, one launch (start us, length us, event | category | flops | bytes accessed | tf_op | source)
XLA Modules:
  0.0 253.8 jit_solution(9579569075582237791)
XLA Ops:
  0.0 0.7 select_convert_fusion
  0.7 1.3 maximum_bitcast_fusion.mine
  2.0 63.8 %front.1 = (f32[4,8,512]{2,1,0:T(8,128)}, bf16[2048,1088]{1,0:T(8,128)(2,1)}, f32[512,2048]{1,0:T(8,128)}, f32[512,2048]{1,0:T(8,128)}, bf16[512,2048]{1,0:T(8,1...) custom-call(bf16[512,2048]{1,0:T(8,128)(2,1)} %x0.1, f32[8,512]{1,0:T(8,128)} %maximum_bitcast_fusion.mine, ...), custom_call_target="tpu_custom_call" | custom-call | flops 35433480192 | bytes 34603008 | tf_op jit(solution)/shard_map/front/pallas_call | solution.py:173
  65.9 72.9 %up.1 = (bf16[15,288,1408]{2,1,0:T(8,128)(2,1)}, f32[15,288,128]{2,1,0:T(8,128)}) custom-call(bf16[512,2048]{1,0:T(8,128)(2,1)} %x0.1, bf16[512,2048]{1,0:T(8,128)(2,1)} %get-tuple-element.15.x1, bf16[512,2048]{1,0:T(8,128)(2,1)} %get-tuple-element.16.x2, bf16[512,2048]{1,0:T(8,128)(2,1)} %get-tuple-element.17.x3, f32[4,8,512]{2,1,0:T(8,128)} %get-tuple-element.18.cx, ...), custom_call_target="tpu_custom_call" | custom-call | flops 49828331520 | bytes 173015040 | tf_op jit(solution)/shard_map/up/pallas_call | solution.py:273
  138.8 111.9 %route.1 = bf16[512,2048]{1,0:T(8,128)(2,1)} custom-call(bf16[2048,1088]{1,0:T(8,128)(2,1)} %get-tuple-element.14.g, f32[15,288,128]{2,1,0:T(8,128)} %get-tuple-element.19.gs, bf16[15,288,1408]{2,1,0:T(8,128)(2,1)} %get-tuple-element.20.h, bf16[15,1408,2048]{2,1,0:T(8,128)(2,1)} %w2.3, f32[512,2048]{1,0:T(8,128)} %get-tuple-element.21.base, ...), custom_call_target="tpu_custom_call" | custom-call | flops 52294582272 | bytes 98672640 | tf_op jit(solution)/shard_map/route/pallas_call | solution.py:475
  250.6 3.2 %copy.12 = bf16[512,2048]{1,0:T(8,128)(2,1)} copy(bf16[512,2048]{1,0:T(8,128)(2,1)} %route.1) | data formatting | bytes 4194304

commit v6 on v5

--- a/solution.py
+++ b/solution.py
@@ -517,8 +517,11 @@
         tok, d = x.shape
         el = w1.shape[0]
         kt = -(-el * CAP // 16) * 16
-        code = jnp.where(slot >= 0, idx * 128 + slot, -1).astype(jnp.float32)
-        mine = jnp.concatenate([code, g], axis=1).T
+        wide = lambda a, lo: jnp.pad(a, ((0, 0), (lo, 4 - lo)))
+        kept = wide(slot, 0) >= 0
+        head = jnp.where(kept, wide(idx, 0) * 128 + wide(slot, 0), -1).astype(jnp.float32)
+        lane = lax.broadcasted_iota(jnp.int32, head.shape, 1)
+        mine = jnp.where(lane < 4, head, wide(g, 4)).T
         cx, gm, base, sy, xc, xx, xxc = _front(x, mine, ws1, ws3, ws2, el, kt)
         h, gs = _up((x, xc, xx, xxc), cx, w1, w3)
         return _route(gm, gs, h, w2, base, sy)

time: 254 us -> 253 us (level)
  no operation moved by 1% of the time
where the time goes in v6:
time: 253 us
  Pallas kernels  249 us (98%)
  local copies, waits for them, and re-layouts  3.16 us (1%)
    pallas_call x1, Pallas kernels, _route(): pl.pallas_call(functools.partial(_route_kernel, el, tok, cols), out_shape...  112 us
    pallas_call x1, Pallas kernels, _up(): pl.pallas_call(functools.partial(_up_kernel, el), grid=(el,), out_shape=[...  72.9 us
    pallas_call x1, Pallas kernels, _front(): pl.pallas_call(functools.partial(_front_kernel, el, kt), out_shape=[jax.S...  63.8 us

profile of v6, /device:TPU:0, one launch (start us, length us, event | category | flops | bytes accessed | tf_op | source)
XLA Modules:
  0.0 253.1 jit_solution(13078112084403406358)
XLA Ops:
  0.0 1.4 fusion.3.mine
  1.4 63.8 %front.1 = (f32[4,8,512]{2,1,0:T(8,128)}, bf16[2048,1088]{1,0:T(8,128)(2,1)}, f32[512,2048]{1,0:T(8,128)}, f32[512,2048]{1,0:T(8,128)}, bf16[512,2048]{1,0:T(8,1...) custom-call(bf16[512,2048]{1,0:T(8,128)(2,1)} %x0.1, f32[8,512]{1,0:T(8,128)} %fusion.3.mine, ...), custom_call_target="tpu_custom_call" | custom-call | flops 35433480192 | bytes 34603008 | tf_op jit(solution)/shard_map/front/pallas_call | solution.py:173
  65.3 72.9 %up.1 = (bf16[15,288,1408]{2,1,0:T(8,128)(2,1)}, f32[15,288,128]{2,1,0:T(8,128)}) custom-call(bf16[512,2048]{1,0:T(8,128)(2,1)} %x0.1, bf16[512,2048]{1,0:T(8,128)(2,1)} %get-tuple-element.15.x1, bf16[512,2048]{1,0:T(8,128)(2,1)} %get-tuple-element.16.x2, bf16[512,2048]{1,0:T(8,128)(2,1)} %get-tuple-element.17.x3, f32[4,8,512]{2,1,0:T(8,128)} %get-tuple-element.18.cx, ...), custom_call_target="tpu_custom_call" | custom-call | flops 49828331520 | bytes 173015040 | tf_op jit(solution)/shard_map/up/pallas_call | solution.py:273
  138.1 111.8 %route.1 = bf16[512,2048]{1,0:T(8,128)(2,1)} custom-call(bf16[2048,1088]{1,0:T(8,128)(2,1)} %get-tuple-element.14.g, f32[15,288,128]{2,1,0:T(8,128)} %get-tuple-element.19.gs, bf16[15,288,1408]{2,1,0:T(8,128)(2,1)} %get-tuple-element.20.h, bf16[15,1408,2048]{2,1,0:T(8,128)(2,1)} %w2.3, f32[512,2048]{1,0:T(8,128)} %get-tuple-element.21.base, ...), custom_call_target="tpu_custom_call" | custom-call | flops 52294582272 | bytes 98672640 | tf_op jit(solution)/shard_map/route/pallas_call | solution.py:475
  250.0 3.2 %copy.12 = bf16[512,2048]{1,0:T(8,128)(2,1)} copy(bf16[512,2048]{1,0:T(8,128)(2,1)} %route.1) | data formatting | bytes 4194304
  (1 shorter events, 0.0 us)
